TPU v7x, 32 devices: a whole 2x2x4 slice. The times are simulated.
32 devices in a mesh: rad: 8 (over y, x, core), ang: 4 (over z).
Axes of the slice: x: 2, y: 2, z: 4, core: 2. Of those that a mesh axis runs over, the one named last changes fastest.
Arguments:
- density: float32 [3, 512, 128, 512], P(None, 'rad', 'ang'), may hold values from -13 to 13
Outputs:
- potential: float32 [3, 512, 128, 512], P(None, 'rad', 'ang')
All inputs are finite; a program needn't handle non-finite values.
Results may differ from a plain program's by a relative error of at most 0.0003.
Values sent between devices are 32-bit elements; how exact they have to be, the bound alone decides.
A program may use at most 128 MiB of HBM per device.

v0:
```python
import math
import jax
import jax.numpy as jnp
import numpy as np
from jax import lax
from jax.sharding import PartitionSpec as P

LMAX = 12
INNER = 0.5
COUPLING = 2000.0


def entering(part, axis, combine, identity, reverse):
    count = lax.axis_size(axis)
    place = lax.axis_index(axis)
    ahead = count - 1 - place if reverse else place
    gathered = lax.all_gather(part, axis)
    state = jnp.zeros_like(part) + jnp.asarray(identity, part.dtype)

    def one(turn, state):
        source = count - 1 - turn if reverse else turn
        return combine(state, lax.dynamic_index_in_dim(gathered, source, 0, False))

    return lax.fori_loop(0, ahead, one, state)


def legendre_table(polar_angle):
    cos_theta = jnp.cos(polar_angle)
    sine_theta = jnp.sin(polar_angle)
    values_lm = {}
    values_lm[0, 0] = jnp.full_like(polar_angle, 1.0 / math.sqrt(4.0 * math.pi))
    for m in range(1, LMAX + 1):
        values_lm[m, m] = (
            math.sqrt((2.0 * m + 1.0) / (2.0 * m)) * sine_theta * values_lm[m - 1, m - 1]
        )
    for m in range(0, LMAX):
        values_lm[m + 1, m] = math.sqrt(2.0 * m + 3.0) * cos_theta * values_lm[m, m]
    for m in range(0, LMAX + 1):
        for l in range(m + 2, LMAX + 1):
            coef_a = math.sqrt((4.0 * l * l - 1.0) / (l * l - m * m))
            coef_b = math.sqrt(((l - 1.0) ** 2 - m * m) / (4.0 * (l - 1.0) ** 2 - 1.0))
            values_lm[l, m] = coef_a * (
                cos_theta * values_lm[l - 1, m] - coef_b * values_lm[l - 2, m]
            )
    degree_rows = []
    for l in range(LMAX + 1):
        columns = []
        for k in range(2 * LMAX + 1):
            m = (k + 1) // 2
            columns.append(values_lm[l, m] if m <= l else jnp.zeros_like(polar_angle))
        degree_rows.append(jnp.stack(columns, -1))
    return jnp.stack(degree_rows, 1)


def fourier_table(phi_cells):
    azimuth = jnp.arange(phi_cells, dtype=jnp.float32) * (2.0 * math.pi / phi_cells)
    column = jnp.arange(2 * LMAX + 1)
    order_m = ((column + 1) // 2).astype(jnp.float32)
    phase = azimuth[:, None] * order_m[None, :]
    root_two = math.sqrt(2.0)
    return jnp.where(
        column[None, :] == 0,
        jnp.ones_like(phase),
        jnp.where(column[None, :] % 2 == 1, root_two * jnp.cos(phase), root_two * jnp.sin(phase)),
    )


def slot_selector():
    width = 2 * LMAX + 1
    used = [l * width + k for l in range(LMAX + 1) for k in range(width) if (k + 1) // 2 <= l]
    table = np.zeros(((LMAX + 1) * width, len(used)), np.float32)
    table[np.array(used), np.arange(len(used))] = 1.0
    return jnp.asarray(table)


def add_terms(earlier, later):
    return jax.tree.map(jnp.add, earlier, later)


def body(density):
    snapshots, shells, theta_rows, phi_cells = density.shape
    width = 2 * LMAX + 1
    total_shells = shells * lax.axis_size("rad")
    total_rows = theta_rows * lax.axis_size("ang")
    row_index = lax.axis_index("ang") * theta_rows + jnp.arange(theta_rows, dtype=jnp.int32)
    polar_angle = (row_index.astype(jnp.float32) + 0.5) * (math.pi / total_rows)
    legendre = legendre_table(polar_angle)
    weights = jnp.sin(polar_angle) * (math.pi / total_rows) * (2.0 * math.pi / phi_cells)
    fourier = fourier_table(phi_cells)
    spacing = (1.0 - INNER) / total_shells
    shell_index = lax.axis_index("rad") * shells + jnp.arange(shells, dtype=jnp.int32)
    radius = INNER + (shell_index.astype(jnp.float32) + 0.5) * spacing
    azimuthal = jnp.dot(
        density.reshape(snapshots * shells * theta_rows, phi_cells),
        fourier,
        precision=lax.Precision.HIGHEST,
        preferred_element_type=jnp.float32,
    )
    azimuthal = azimuthal.reshape(snapshots, shells, theta_rows, width)
    partial_moments = jnp.einsum(
        "frtk,tlk->frlk",
        azimuthal,
        legendre * weights[:, None, None],
        precision=lax.Precision.HIGHEST,
    )
    selector = slot_selector()
    packed = jnp.dot(
        partial_moments.reshape(snapshots * shells, (LMAX + 1) * width),
        selector,
        precision=lax.Precision.HIGHEST,
        preferred_element_type=jnp.float32,
    )
    summed = lax.psum(packed, "ang")
    moments = jnp.dot(
        summed, selector.T, precision=lax.Precision.HIGHEST, preferred_element_type=jnp.float32
    ).reshape(snapshots, shells, LMAX + 1, width)
    degree = jnp.arange(LMAX + 1, dtype=jnp.float32)
    inner_terms = moments * (radius[:, None] ** (degree + 2.0) * spacing)[None, :, :, None]
    outer_terms = moments * (radius[:, None] ** (1.0 - degree) * spacing)[None, :, :, None]
    inner_total = jnp.sum(inner_terms, 1)
    outer_total = jnp.sum(outer_terms, 1)
    zeros_block = jnp.zeros_like(inner_total)
    from_below = entering(inner_total, "rad", add_terms, zeros_block, False)
    from_above = entering(outer_total, "rad", add_terms, zeros_block, True)
    inner_sum = from_below[:, None] + jnp.cumsum(inner_terms, 1) - 0.5 * inner_terms
    outer_sum = (
        from_above[:, None]
        + jnp.flip(jnp.cumsum(jnp.flip(outer_terms, 1), 1), 1)
        - 0.5 * outer_terms
    )
    factor = (-COUPLING * 4.0 * math.pi / (2.0 * degree + 1.0))[None, None, :, None]
    coefficient = factor * (
        (radius[:, None] ** (-(degree[None, :] + 1.0)))[None, :, :, None] * inner_sum
        + (radius[:, None] ** degree[None, :])[None, :, :, None] * outer_sum
    )
    spread = jnp.einsum("frlk,tlk->frtk", coefficient, legendre, precision=lax.Precision.HIGHEST)
    potential = jnp.dot(
        spread.reshape(snapshots * shells * theta_rows, width),
        fourier.T,
        precision=lax.Precision.HIGHEST,
        preferred_element_type=jnp.float32,
    )
    return potential.reshape(snapshots, shells, theta_rows, phi_cells)


def solution(mesh):
    return jax.shard_map(
        body,
        mesh=mesh,
        in_specs=(P(None, "rad", "ang", None),),
        out_specs=P(None, "rad", "ang", None),
        check_vma=False,
    )
```

profile of v0, /device:TPU:0, one launch (start us, length us, event | category | flops | bytes accessed | tf_op | source)
XLA Modules:
  0.0 137.9 jit_solution(15535400083472716511)
XLA Ops:
  12.8 15.4 %convolution_bitcast_fusion = f32[6144,25]{0,1:T(8,128)S(1)} fusion(f32[6144,512]{1,0:T(8,128)} %bitcast.64, f32[25]{0:T(128)S(1)} %fusion.29, f32[512]{0:T(512)S(1)} %iota_multiply_fusion, pred[25]{0:T(512)(128)(4,1)S(1)} %get-tuple-element.109, pred[25]{0:T(512)(128)(4,1)S(1)} %get-tuple-element.110), kind=kOutput, calls=%fused_computation.2 | convolution fusion | flops 943782400 | bytes 13199510 | tf_op jit(solution)/shard_map/dot_general | solution.py:93
  28.2 0.8 reshape.1258
  29.0 1.0 stack.74
  30.0 5.8 %convolution_bitcast_fusion.2 = f32[3,64,13,25]{1,2,0,3:T(8,128)S(1)} fusion(f32[3,64,32,25]{2,1,0,3:T(8,128)S(1)} %reshape.1258, f32[32,13,25]{0,1,2:T(8,128)S(1)} %stack.74, f32[32]{0:T(128)} %sine_multiply_fusion), kind=kOutput, calls=%fused_computation.8 | convolution fusion | flops 23972000 | bytes 905728 | tf_op jit(solution)/shard_map/frtk,tlk->frlk/dot_general | solution.py:100
  36.8 1.5 %fusion.37 = f32[192,169]{0,1:T(8,128)} fusion(f32[192,325]{0,1:T(8,128)S(1)} %reshape.1259, f32[325,169]{1,0:T(8,128)S(1)} %copy-done), kind=kOutput, calls=%fused_computation.198 | convolution fusion | flops 126547200 | bytes 599092 | tf_op jit(solution)/shard_map/dot_general | solution.py:107
  38.6 37.2 %all-reduce.2.cloned.1.call-done = f32[192,169]{0,1:T(8,128)} async-done(((f32[192,169]{0,1:T(8,128)}), f32[192,169]{0,1:T(8,128)}) %all-reduce.2.cloned.1.call-update) | async-done | bytes 129808 | tf_op jit(solution)/shard_map/psum | solution.py:113
  75.8 1.4 fusion.38
  78.6 10.2 %all-gather = f32[24,13,25]{2,1,0:T(8,128)} all-gather(f32[3,13,25]{2,1,0:T(8,128)S(1)} %get-tuple-element.86), channel_id=2, replica_groups=mesh['rad'=8,'ang'=4] {'rad'}, dimensions={0}, use_global_device_ids=true | all-gather | bytes 35100 | tf_op jit(solution)/shard_map/all_gather | solution.py:17
  88.8 14.3 %all-gather.1 = f32[24,13,25]{2,1,0:T(8,128)} all-gather(f32[3,13,25]{2,1,0:T(8,128)S(1)} %get-tuple-element.87), channel_id=3, replica_groups=mesh['rad'=8,'ang'=4] {'rad'}, dimensions={0}, use_global_device_ids=true | all-gather | bytes 35100 | tf_op jit(solution)/shard_map/all_gather | solution.py:17
  103.1 5.2 %while.23 = (s32[]{:T(128)}, f32[3,13,25]{2,1,0:T(8,128)S(1)}, s32[]{:T(128)}, f32[8,3,13,25]{3,2,1,0:T(8,128)}, s32[]{:T(128)}, /*index=5*/s32[]{:T(128)}, s32[]{:T(128)}, s32[]{:T(128)}) while((s32[]{:T(128)}, f32[3,13,25]{2,1,0:T(8,128)S(1)}, s32[]{:T(128)}, f32[8,3,13,25]{3,2,1,0:T(8,128)}, s32[]{:T(128)}, /*index=5*/s32[]{:T(128)}, ...), condition=%wide.region_7.8_spmd, body=%wide.region_6.7_spmd.sunk | while | flops 981 | bytes 11843 | solution.py:24
  103.1 0.7 bitcast_add_fusion.5
  103.8 0.7 bitcast_add_fusion.5
  104.6 0.7 bitcast_add_fusion.5
  105.3 0.7 bitcast_add_fusion.5
  106.1 0.7 bitcast_add_fusion.5
  106.8 0.7 bitcast_add_fusion.5
  107.5 0.7 bitcast_add_fusion.5
  108.3 1.2 rev.7
  109.5 1.5 %fusion.36 = f32[3,64,13,25]{3,2,1,0:T(8,128)S(1)} fusion(f32[3,64,13,25]{3,2,1,0:T(8,128)} %rev.7), kind=kOutput, calls=%fused_computation.197 | output fusion | flops 3931200 | bytes 499200 | tf_op jit(solution)/shard_map/jit(cumsum)/reduce_window_sum | solution.py:128
  111.1 0.8 add_multiply_fusion
  111.9 0.8 copy.35
  112.7 2.2 %convolution_bitcast_fusion.1 = f32[3,64,32,25]{1,2,0,3:T(8,128)} fusion(f32[3,64,13,25]{1,2,0,3:T(8,128)S(1)} %copy.35, f32[32,13,25]{0,1,2:T(8,128)S(1)} %stack.74), kind=kOutput, calls=%fused_computation.4 | convolution fusion | flops 23961600 | bytes 905600 | tf_op jit(solution)/shard_map/frlk,tlk->frtk/dot_general | solution.py:136
  114.9 2.9 %copy.36 = f32[3,64,32,25]{3,2,1,0:T(8,128)S(1)} copy(f32[3,64,32,25]{1,2,0,3:T(8,128)} %convolution_bitcast_fusion.1) | data formatting | bytes 1228800 | tf_op jit(solution)/shard_map/frlk,tlk->frtk/transpose | solution.py:136
  117.8 13.2 %fusion.14 = f32[3,64,32,512]{3,2,1,0:T(8,128)} fusion(f32[3,64,32,25]{3,2,1,0:T(8,128)S(1)} %copy.36, f32[25]{0:T(128)S(1)} %fusion.29, f32[512]{0:T(512)S(1)} %iota_multiply_fusion, pred[25]{0:T(512)(128)(4,1)S(1)} %copy-done.2, pred[25]{0:T(512)(128)(4,1)S(1)} %copy-done.4), kind=kOutput, calls=%fused_computation.23 | convolution fusion | flops 943782400 | bytes 13199510 | tf_op jit(solution)/shard_map/dot_general | solution.py:137
  (102 shorter events, 8.5 us)
Async XLA Ops:
  6.5 69.3 %all-reduce.2.cloned.1.call-start = ((), (), s32[]{:S(2)}) async-start(), calls=%async_computation | async-start | bytes 360448 | tf_op jit(solution)/shard_map/psum | solution.py:113
  10.1 18.1 %copy-start.1 = (pred[25]{0:T(512)(128)(4,1)}, pred[25]{0:T(512)(128)(4,1)S(1)}, u32[]{:S(2)}) copy-start(pred[25]{0:T(512)(128)(4,1)S(1)} %get-tuple-element.109) | copy-start | bytes 79
  10.2 18.1 %copy-start.3 = (pred[25]{0:T(512)(128)(4,1)}, pred[25]{0:T(512)(128)(4,1)S(1)}, u32[]{:S(2)}) copy-start(pred[25]{0:T(512)(128)(4,1)S(1)} %get-tuple-element.110) | copy-start | bytes 79
  35.8 1.0 copy-start
  114.9 2.9 %copy-start.2 = (pred[25]{0:T(512)(128)(4,1)S(1)}, pred[25]{0:T(512)(128)(4,1)}, u32[]{:S(2)}) copy-start(pred[25]{0:T(512)(128)(4,1)} %copy-done.1) | copy-start | bytes 79
  114.9 2.9 %copy-start.4 = (pred[25]{0:T(512)(128)(4,1)S(1)}, pred[25]{0:T(512)(128)(4,1)}, u32[]{:S(2)}) copy-start(pred[25]{0:T(512)(128)(4,1)} %copy-done.3) | copy-start | bytes 79
Sparse Core Ops, SparseCore 0:
  38.4 37.3 all-reduce.1
where the time goes:
time: 139 us; the launch traced here: 138 us
  matrix products  39.5 us (28%)
  waiting for transfers between devices  37.2 us (27%)
  blocking collectives  24.5 us (18%)
  between operations  13.9 us (10%)
  other arithmetic  11.7 us (8%)
  local copies, waits for them, and re-layouts  11 us (8%)
    psum x1, waiting for transfers between devices, body(): summed = lax.psum(packed, 'ang')  37.2 us
    all_gather x2, blocking collectives, entering(): gathered = lax.all_gather(part, axis)  24.5 us
    dot_general x1, matrix products, body(): jnp.dot(density.reshape(snapshots * shells * theta_rows, phi_cells), four...  15.4 us
    dot_general x1, matrix products, body(): jnp.dot(spread.reshape(snapshots * shells * theta_rows, width), fourier.T...  13.2 us
    dot_general x1, matrix products, body(): jnp.einsum('frtk,tlk->frlk', azimuthal, legendre * weights[:, None, None]...  5.83 us
    add x7, other arithmetic, add_terms(): return jax.tree.map(jnp.add, earlier, later)  5.19 us
    transpose x1, local copies, waits for them, and re-layouts, body(): jnp.einsum('frlk,tlk->frtk', coefficient, legendre, precision=lax.Precisi...  2.88 us
  transfers between devices with their start and end apart: 1, of which 1 were waited for; matrix products, arithmetic and copies ran while one was open for 0% of the time, Pallas kernels for 0%

commit v1 on v0

--- a/solution.py
+++ b/solution.py
@@ -110,7 +110,7 @@
         precision=lax.Precision.HIGHEST,
         preferred_element_type=jnp.float32,
     )
-    summed = lax.psum(packed, "ang")
+    summed = jnp.sum(lax.all_gather(packed, "ang"), axis=0)
     moments = jnp.dot(
         summed, selector.T, precision=lax.Precision.HIGHEST, preferred_element_type=jnp.float32
     ).reshape(snapshots, shells, LMAX + 1, width)

time: 139 us -> 137 us (0.986)
  waiting for transfers between devices: 37.2 us -> 0 us
  other arithmetic: 11.7 us -> 44.6 us
  blocking collectives: 24.5 us -> 39.4 us
  between operations: 13.9 us -> 0.69 us
  local copies, waits for them, and re-layouts: 11 us -> 13.7 us
    psum x1 -> x0, waiting for transfers between devices: 37.2 us -> none  [body(): summed = lax.psum(packed, 'ang')]
    all_gather x0 -> x1, blocking collectives: none -> 20.8 us  [body(): summed = jnp.sum(lax.all_gather(packed, 'ang'), axis=0)]
    another operation x1, other arithmetic: 0.84 us -> 19.7 us  [body(): jnp.cumsum(inner_terms, 1)]
    another operation x1, other arithmetic: 1.53 us -> 19.7 us  [body(): jnp.cumsum(jnp.flip(outer_terms, 1), 1)]
    all_gather x2, blocking collectives: 24.5 us -> 18.6 us  [entering(): gathered = lax.all_gather(part, axis)]
    add x7, other arithmetic: 5.19 us -> 0.07 us  [add_terms(): return jax.tree.map(jnp.add, earlier, later)]
    another operation x4 -> x6, local copies, waits for them, and re-layouts: 0.01 us -> 1.98 us  [the longest x1 1.38 us: body(): jnp.cumsum(inner_terms, 1)]
    mul x0 -> x1, other arithmetic: none -> 1.57 us  [body(): factor * ((radius[:, None] ** (-(degree[None, :] + 1.0)))[None, :, :, Non...]
  transfers between devices with their start and end apart: 1 -> 0, of which waited for: 1 -> 0; matrix products, arithmetic and copies ran while one was open for 0% -> 0% of each run, Pallas kernels for 0% -> 0%
where the time goes in v1:
time: 137 us
  other arithmetic  44.6 us (33%)
  blocking collectives  39.4 us (29%)
  matrix products  38.6 us (28%)
  local copies, waits for them, and re-layouts  13.7 us (10%)
    all_gather x1, blocking collectives, body(): summed = jnp.sum(lax.all_gather(packed, 'ang'), axis=0)  20.8 us
    another operation x1, other arithmetic, body(): jnp.cumsum(jnp.flip(outer_terms, 1), 1)  19.7 us
    another operation x1, other arithmetic, body(): jnp.cumsum(inner_terms, 1)  19.7 us
    all_gather x2, blocking collectives, entering(): gathered = lax.all_gather(part, axis)  18.6 us
    dot_general x1, matrix products, body(): jnp.dot(density.reshape(snapshots * shells * theta_rows, phi_cells), four...  15.3 us
    dot_general x1, matrix products, body(): jnp.dot(spread.reshape(snapshots * shells * theta_rows, width), fourier.T...  13.2 us
    dot_general x1, matrix products, body(): jnp.einsum('frtk,tlk->frlk', azimuthal, legendre * weights[:, None, None]...  5.17 us
    transpose x1, local copies, waits for them, and re-layouts, body(): jnp.einsum('frlk,tlk->frtk', coefficient, legendre, precision=lax.Precisi...  2.89 us

profile of v1, /device:TPU:0, one launch (start us, length us, event | category | flops | bytes accessed | tf_op | source)
XLA Modules:
  0.0 137.2 jit_solution(6210015244346280767)
XLA Ops:
  0.1 0.5 add_divide_fusion
  3.8 0.3 stack.70
  6.7 1.0 stack.74
  7.6 15.3 %convolution_bitcast_fusion = f32[6144,25]{0,1:T(8,128)S(1)} fusion(f32[6144,512]{1,0:T(8,128)} %bitcast.70, f32[25]{0:T(128)S(1)} %fusion.26, f32[512]{0:T(512)S(1)} %iota_multiply_fusion, pred[25]{0:T(512)(128)(4,1)S(1)} %get-tuple-element.112, pred[25]{0:T(512)(128)(4,1)S(1)} %get-tuple-element.113), kind=kOutput, calls=%fused_computation.2 | convolution fusion | flops 943782400 | bytes 13199510 | tf_op jit(solution)/shard_map/dot_general | solution.py:93
  23.0 0.8 reshape.1258
  23.8 5.2 %convolution_bitcast_fusion.2 = f32[3,64,13,25]{1,2,0,3:T(8,128)S(1)} fusion(f32[3,64,32,25]{2,1,0,3:T(8,128)S(1)} %reshape.1258, f32[32,13,25]{0,1,2:T(8,128)S(1)} %stack.74, f32[32]{0:T(128)S(1)} %sine_multiply_fusion), kind=kOutput, calls=%fused_computation.4 | convolution fusion | flops 23972000 | bytes 905728 | tf_op jit(solution)/shard_map/frtk,tlk->frlk/dot_general | solution.py:100
  29.2 0.4 reshape.1259
  29.6 0.8 convolution_bitcast_fusion.3
  30.4 20.8 %all-gather.3 = f32[4,192,169]{1,2,0:T(8,128)S(1)} all-gather(f32[1,192,169]{1,2,0:T(8,128)S(1)} %convolution_bitcast_fusion.3), channel_id=2, replica_groups=mesh['rad'=8,'ang'=4] {'ang'}, dimensions={0}, use_global_device_ids=true | all-gather | bytes 648960 | tf_op jit(solution)/shard_map/all_gather | solution.py:113
  51.4 1.7 %fusion.33 = (f32[3,13,25]{2,1,0:T(8,128)S(1)}, f32[3,64,13,25]{1,3,2,0:T(8,128)}, f32[3,13,25]{2,1,0:T(8,128)S(1)}, f32[3,64,13,25]{1,3,2,0:T(8,128)S(1)}) fusion(f32[64,13]{0,1:T(8,128)S(1)} %get-tuple-element.109, f32[64,13]{0,1:T(8,128)S(1)} %get-tuple-element.111, f32[3,64,169,1]{2,1,3,0:T(8,128)S(1)} %bitcast.71, f32[13,25,169,1]{2,1,0,3:T(8,128)S(1)} %copy-done.7), kind=kOutput, calls=%fused_computation.195 | convolution fusion | flops 126794848 | bytes 863148 | tf_op jit(solution)/shard_map/dot_general | solution.py:114
  53.0 9.3 %all-gather.1 = f32[24,13,25]{2,1,0:T(8,128)S(1)} all-gather(f32[3,13,25]{2,1,0:T(8,128)S(1)} %get-tuple-element.102), channel_id=3, replica_groups=mesh['rad'=8,'ang'=4] {'rad'}, dimensions={0}, use_global_device_ids=true | all-gather | bytes 35100 | tf_op jit(solution)/shard_map/all_gather | solution.py:17
  62.3 9.4 %all-gather.2 = f32[24,13,25]{2,1,0:T(8,128)S(1)} all-gather(f32[3,13,25]{2,1,0:T(8,128)S(1)} %get-tuple-element.106), channel_id=4, replica_groups=mesh['rad'=8,'ang'=4] {'rad'}, dimensions={0}, use_global_device_ids=true | all-gather | bytes 35100 | tf_op jit(solution)/shard_map/all_gather | solution.py:17
  71.9 0.8 rev.7
  72.8 0.8 copy.56
  73.5 19.7 %fusion.36 = f32[3,64,13,25]{3,2,1,0:T(8,128)S(1)} fusion(f32[3,64,13,25]{3,2,1,0:T(8,128)S(1)} %copy.56), kind=kOutput, calls=%fused_computation.198 | output fusion | flops 3931200 | bytes 499200 | tf_op jit(solution)/shard_map/jit(cumsum)/reduce_window_sum | solution.py:128
  93.2 0.6 copy.57
  93.8 1.3 rev.8
  95.1 0.8 copy.54
  95.9 19.7 %fusion.35 = f32[3,64,13,25]{3,2,1,0:T(8,128)S(1)} fusion(f32[3,64,13,25]{3,2,1,0:T(8,128)S(1)} %copy.54), kind=kOutput, calls=%fused_computation.197 | output fusion | flops 3931200 | bytes 499200 | tf_op jit(solution)/shard_map/jit(cumsum)/reduce_window_sum | solution.py:125
  115.6 1.4 %copy.55 = f32[3,64,13,25]{1,3,2,0:T(8,128)} copy(f32[3,64,13,25]{3,2,1,0:T(8,128)S(1)} %fusion.35) | data formatting | bytes 499200 | tf_op jit(solution)/shard_map/jit(cumsum)/reduce_window_sum | solution.py:125
  117.0 1.6 %add_multiply_fusion = f32[3,64,13,25]{1,3,2,0:T(8,128)S(1)} fusion(f32[3,64,13,25]{1,3,2,0:T(8,128)S(1)} %copy-done.1, f32[3,64,13,25]{1,3,2,0:T(8,128)S(1)} %copy-done.4, f32[3,64,13,25]{1,3,2,0:T(8,128)S(1)} %copy-done.3, f32[3,64,13,25]{1,3,2,0:T(8,128)} %copy.55, f32[3,13,25]{2,1,0:T(8,128)S(1)} %get-tuple-element.85, ...), kind=kLoop, calls=%fused_computation.6 | loop fusion | flops 624000 | bytes 1262508 | tf_op jit(solution)/shard_map/mul | solution.py:132
  118.6 2.5 %convolution_bitcast_fusion.1 = f32[3,64,32,25]{1,2,0,3:T(8,128)} fusion(f32[3,64,13,25]{1,3,2,0:T(8,128)S(1)} %add_multiply_fusion, f32[32,13,25]{0,1,2:T(8,128)S(1)} %copy-done.6), kind=kOutput, calls=%fused_computation.3 | convolution fusion | flops 23961600 | bytes 905600 | tf_op jit(solution)/shard_map/frlk,tlk->frtk/dot_general | solution.py:136
  121.1 2.9 %copy.59 = f32[3,64,32,25]{3,2,1,0:T(8,128)S(1)} copy(f32[3,64,32,25]{1,2,0,3:T(8,128)} %convolution_bitcast_fusion.1) | data formatting | bytes 1228800 | tf_op jit(solution)/shard_map/frlk,tlk->frtk/transpose | solution.py:136
  124.0 13.2 %fusion.11 = f32[3,64,32,512]{3,2,1,0:T(8,128)} fusion(f32[3,64,32,25]{3,2,1,0:T(8,128)S(1)} %copy.59, f32[25]{0:T(128)S(1)} %copy-done.12, f32[512]{0:T(512)S(1)} %copy-done.10, pred[25]{0:T(512)(128)(4,1)S(1)} %copy-done.14, pred[25]{0:T(512)(128)(4,1)S(1)} %copy-done.16), kind=kOutput, calls=%fused_computation.21 | convolution fusion | flops 943782400 | bytes 13199510 | tf_op jit(solution)/shard_map/dot_general | solution.py:137
  (128 shorter events, 6.2 us)
Async XLA Ops:
  0.0 22.9 %copy-start.11 = (f32[25]{0:T(128)}, f32[25]{0:T(128)S(1)}, u32[]{:S(2)}) copy-start(f32[25]{0:T(128)S(1)} %fusion.26) | copy-start | bytes 304
  3.7 19.3 %copy-start.13 = (pred[25]{0:T(512)(128)(4,1)}, pred[25]{0:T(512)(128)(4,1)S(1)}, u32[]{:S(2)}) copy-start(pred[25]{0:T(512)(128)(4,1)S(1)} %get-tuple-element.112) | copy-start | bytes 79
  3.7 19.3 %copy-start.15 = (pred[25]{0:T(512)(128)(4,1)}, pred[25]{0:T(512)(128)(4,1)S(1)}, u32[]{:S(2)}) copy-start(pred[25]{0:T(512)(128)(4,1)S(1)} %get-tuple-element.113) | copy-start | bytes 79
  3.7 19.3 %copy-start.9 = (f32[512]{0:T(512)}, f32[512]{0:T(512)S(1)}, u32[]{:S(2)}) copy-start(f32[512]{0:T(512)S(1)} %iota_multiply_fusion) | copy-start | bytes 6148
  7.6 16.2 %copy-start.5 = (f32[32,13,25]{0,1,2:T(8,128)}, f32[32,13,25]{0,1,2:T(8,128)S(1)}, u32[]{:S(2)}) copy-start(f32[32,13,25]{0,1,2:T(8,128)S(1)} %stack.74) | copy-start | bytes 124804
  23.8 5.8 %copy-start.8 = (f32[325,169]{1,0:T(8,128)S(1)}, f32[325,169]{1,0:T(8,128)}, u32[]{:S(2)}) copy-start(f32[325,169]{1,0:T(8,128)} %constant.479.clone) | copy-start | bytes 659104
  29.0 22.4 %copy-start.7 = (f32[13,25,169,1]{2,1,0,3:T(8,128)S(1)}, f32[13,25,169,1]{2,1,0,3:T(8,128)}, u32[]{:S(2)}) copy-start(f32[13,25,169,1]{2,1,0,3:T(8,128)} %constant.481) | copy-start | bytes 659104
  53.0 18.9 %copy-start = (f32[3,64,13,25]{1,3,2,0:T(8,128)}, f32[3,64,13,25]{1,3,2,0:T(8,128)S(1)}, u32[]{:S(2)}) copy-start(f32[3,64,13,25]{1,3,2,0:T(8,128)S(1)} %get-tuple-element.107) | copy-start | bytes 748804
  93.2 1.9 %copy-start.2 = (f32[3,64,13,25]{1,3,2,0:T(8,128)S(1)}, f32[3,64,13,25]{1,3,2,0:T(8,128)}, u32[]{:S(2)}) copy-start(f32[3,64,13,25]{1,3,2,0:T(8,128)} %get-tuple-element.103) | copy-start | bytes 748804
  115.5 1.4 %copy-start.1 = (f32[3,64,13,25]{1,3,2,0:T(8,128)S(1)}, f32[3,64,13,25]{1,3,2,0:T(8,128)}, u32[]{:S(2)}) copy-start(f32[3,64,13,25]{1,3,2,0:T(8,128)} %copy-done) | copy-start | bytes 748804
  115.5 1.4 %copy-start.3 = (f32[3,64,13,25]{1,3,2,0:T(8,128)S(1)}, f32[3,64,13,25]{1,3,2,0:T(8,128)}, u32[]{:S(2)}) copy-start(f32[3,64,13,25]{1,3,2,0:T(8,128)} %get-tuple-element.103) | copy-start | bytes 748804
  115.6 1.4 %copy-start.4 = (f32[3,64,13,25]{1,3,2,0:T(8,128)S(1)}, f32[3,64,13,25]{1,3,2,0:T(8,128)}, u32[]{:S(2)}) copy-start(f32[3,64,13,25]{1,3,2,0:T(8,128)} %rev.8) | copy-start | bytes 748804
  117.0 1.6 %copy-start.6 = (f32[32,13,25]{0,1,2:T(8,128)S(1)}, f32[32,13,25]{0,1,2:T(8,128)}, u32[]{:S(2)}) copy-start(f32[32,13,25]{0,1,2:T(8,128)} %copy-done.5) | copy-start | bytes 124804
  121.1 2.9 %copy-start.10 = (f32[512]{0:T(512)S(1)}, f32[512]{0:T(512)}, u32[]{:S(2)}) copy-start(f32[512]{0:T(512)} %copy-done.9) | copy-start | bytes 6148
  121.1 2.9 %copy-start.12 = (f32[25]{0:T(128)S(1)}, f32[25]{0:T(128)}, u32[]{:S(2)}) copy-start(f32[25]{0:T(128)} %copy-done.11) | copy-start | bytes 304
  121.1 2.9 %copy-start.14 = (pred[25]{0:T(512)(128)(4,1)S(1)}, pred[25]{0:T(512)(128)(4,1)}, u32[]{:S(2)}) copy-start(pred[25]{0:T(512)(128)(4,1)} %copy-done.13) | copy-start | bytes 79
  121.1 2.9 %copy-start.16 = (pred[25]{0:T(512)(128)(4,1)S(1)}, pred[25]{0:T(512)(128)(4,1)}, u32[]{:S(2)}) copy-start(pred[25]{0:T(512)(128)(4,1)} %copy-done.15) | copy-start | bytes 79
